TPU v7x, 32 devices: a whole 2x2x4 slice. The times are simulated.
32 devices in a mesh: expert: 4 (over y, x), tensor: 4 (over z), rep: 2 (over core).
Axes of the slice: x: 2, y: 2, z: 4, core: 2. Of those that a mesh axis runs over, the one named last changes fastest.
Arguments:
- requests: bfloat16 [512, 1536], P('expert', ('tensor', 'rep')), may hold values from -6 to 6
- expert_ids: int32 [512, 2], P('expert'), may hold values from 0 to 3, all different within a row; in each aligned block of 128 rows (0 to 127, 128 to 255, ...) at most 96 rows name the same one
- gate_values: float32 [512, 2], P('expert'), may hold values from 0.2 to 1
- w_up: bfloat16 [4, 1536, 6144], P(None, 'expert', ('tensor', 'rep')), may hold values from -0.15625 to 0.15625
- w_down: bfloat16 [4, 1536, 6144], P(None, 'expert', ('tensor', 'rep')), may hold values from -0.078125 to 0.078125
- tower_in: bfloat16 [1536, 768], P(('tensor', 'rep')), may hold values from -0.15625 to 0.15625
- tower_bias: float32 [768], replicated, may hold values from -3 to 3
- tower_out: float32 [3, 256], replicated, may hold values from -0.375 to 0.375
- out_bias: float32 [3], replicated, may hold values from -3 to 3
Outputs:
- mixed: bfloat16 [512, 1536], P('expert', ('tensor', 'rep'))
- scores: float32 [3, 512], P(None, ('expert', 'tensor', 'rep'))
Inputs may be any that keep to these rules, and one draw needn't show every extreme that they name: `expert_ids`: each row names two different experts. In the rows of one device (128 requests) no expert is named more than 96 times, a bound that some block reaches.
All inputs are finite; a program needn't handle non-finite values.
Results may differ from a plain program's by a relative error of at most 0.015.
Values may be sent and summed in bfloat16 or wider, within the bound.
No kernel may reach another device: no remote copies, remote signals or barrier semaphores. Data moves between devices by JAX's collectives and lax.ppermute only.
A program may use at most 64 MiB of HBM per device.

v0:
```python
import jax
import jax.numpy as jnp
from jax import lax
from jax.sharding import PartitionSpec as P


def tower_head(pre, tower_bias, tower_out, out_bias):
    active = jax.nn.relu(pre + tower_bias[None, :])
    active = active.reshape(pre.shape[0], tower_out.shape[0], tower_out.shape[1])
    logits = jnp.sum(active * tower_out[None, :, :], axis=2) + out_bias[None, :]
    return jax.nn.sigmoid(logits).T


def per_device(
    requests, expert_ids, gate_values, w_up, w_down, tower_in, tower_bias, tower_out, out_bias
):
    groups = lax.axis_size("expert")
    experts = w_up.shape[0]
    local_experts = experts // groups
    tok_rows = requests.shape[0]
    capacity = 3 * tok_rows // experts
    serve_up, serve_down = (
        lax.all_to_all(w_up, "expert", split_axis=0, concat_axis=1, tiled=True),
        lax.all_to_all(w_down, "expert", split_axis=0, concat_axis=1, tiled=True),
    )
    flat_ids = expert_ids.reshape(-1)
    onehot = (flat_ids[:, None] == jnp.arange(experts, dtype=jnp.int32)[None, :]).astype(jnp.int32)
    before = jnp.cumsum(onehot, axis=0) - onehot
    slot_rank = jnp.sum(before * onehot, axis=1)
    slots = (flat_ids * capacity + slot_rank).reshape(tok_rows, 2)
    slot_index = jnp.arange(experts * capacity, dtype=jnp.int32)
    spread = (
        (slot_index[:, None] == slots[None, :, 0]) | (slot_index[:, None] == slots[None, :, 1])
    ).astype(jnp.bfloat16)
    full_rows = lax.all_gather(requests, ("tensor", "rep"), axis=1, tiled=True)
    outgoing = jnp.dot(spread, full_rows, preferred_element_type=jnp.float32).astype(jnp.bfloat16)
    incoming = lax.all_to_all(outgoing, "expert", split_axis=0, concat_axis=0, tiled=True)
    shaped = incoming.reshape(groups, local_experts, capacity, incoming.shape[1])
    hidden_pre = jnp.einsum("secd,edh->sech", shaped, serve_up, preferred_element_type=jnp.float32)
    hidden = jax.nn.relu(hidden_pre).astype(jnp.bfloat16)
    partial_value = jnp.einsum(
        "sech,edh->secd", hidden, serve_down, preferred_element_type=jnp.float32
    )
    summed = lax.psum_scatter(
        partial_value.astype(jnp.bfloat16), ("tensor", "rep"), scatter_dimension=3, tiled=True
    ).astype(jnp.float32)
    expert_out = summed.astype(jnp.bfloat16).reshape(
        groups * local_experts * capacity, summed.shape[3]
    )
    returned = lax.all_to_all(expert_out, "expert", split_axis=0, concat_axis=0, tiled=True)
    pick_first = (slots[:, 0:1] == slot_index[None, :]).astype(jnp.bfloat16)
    pick_second = (slots[:, 1:2] == slot_index[None, :]).astype(jnp.bfloat16)
    first = jnp.dot(pick_first, returned, preferred_element_type=jnp.float32)
    second = jnp.dot(pick_second, returned, preferred_element_type=jnp.float32)
    mixed = (gate_values[:, 0:1] * first + gate_values[:, 1:2] * second).astype(jnp.bfloat16)
    pre = lax.psum_scatter(
        jnp.dot(mixed, tower_in, preferred_element_type=jnp.float32).astype(jnp.bfloat16),
        ("tensor", "rep"),
        scatter_dimension=0,
        tiled=True,
    ).astype(jnp.float32)
    scores = tower_head(pre, tower_bias, tower_out, out_bias)
    return (mixed, scores)


def solution(mesh):
    in_specs = (
        P("expert", ("tensor", "rep")),
        P("expert", None),
        P("expert", None),
        P(None, "expert", ("tensor", "rep")),
        P(None, "expert", ("tensor", "rep")),
        P(("tensor", "rep"), None),
        P(),
        P(),
        P(),
    )
    out_specs = (P("expert", ("tensor", "rep")), P(None, ("expert", "tensor", "rep")))
    return jax.shard_map(
        per_device, mesh=mesh, in_specs=in_specs, out_specs=out_specs, check_vma=False
    )
```

profile of v0, /device:TPU:0, one launch (start us, length us, event | category | flops | bytes accessed | tf_op | source)
XLA Modules:
  0.0 198.6 jit_solution(8744839714044765721)
XLA Ops:
  7.2 0.8 copy.32
  8.2 0.1 eq.81
  8.3 1.2 reduce-window.6
  10.0 0.1 reduce_sum.21
  10.2 0.7 multiply_add_fusion
  10.9 16.4 %all_gather.3 = bf16[128,1536]{0,1:T(8,128)(2,1)S(1)} all-gather(bf16[128,192]{0,1:T(8,128)(2,1)} %param.9), channel_id=1, replica_groups=mesh['expert'=4,'tensor'=4,'rep'=2] {'tensor','rep'}, dimensions={1}, use_global_device_ids=true | all-gather | bytes 442368 | tf_op jit(solution)/shard_map/all_gather | solution.py:35
  27.3 0.5 convolution_convert_fusion
  27.8 19.8 %all_to_all.39 = bf16[4,96,1536]{2,1,0:T(8,128)(2,1)} all-to-all(bf16[4,96,1536]{2,1,0:T(8,128)(2,1)S(1)} %bitcast.56), channel_id=1, replica_groups=mesh['expert'=4,'tensor'=4,'rep'=2] {'expert'}, dimensions={0} | all-to-all | bytes 2359296 | tf_op jit(solution)/shard_map/all_to_all | solution.py:37
  47.6 30.1 %all_to_all.40 = bf16[4,384,768]{2,1,0:T(8,128)(2,1)S(1)} all-to-all(bf16[4,384,768]{2,1,0:T(8,128)(2,1)S(1)} %copy-done.1), channel_id=1, replica_groups=mesh['expert'=4,'tensor'=4,'rep'=2] {'expert'}, dimensions={0} | all-to-all | bytes 4718592 | tf_op jit(solution)/shard_map/all_to_all | solution.py:23
  77.7 29.5 %all_to_all.41 = bf16[4,384,768]{2,1,0:T(8,128)(2,1)} all-to-all(bf16[4,384,768]{2,1,0:T(8,128)(2,1)S(1)} %copy-done.2), channel_id=1, replica_groups=mesh['expert'=4,'tensor'=4,'rep'=2] {'expert'}, dimensions={0} | all-to-all | bytes 4718592 | tf_op jit(solution)/shard_map/all_to_all | solution.py:24
  107.3 5.5 %fusion = bf16[4,1,96,1536]{3,2,0,1:T(8,128)(2,1)} fusion(bf16[1536,768,1]{1,0,2:T(8,128)(2,1)} %bitcast.58, bf16[4,96,1536]{2,1,0:T(8,128)(2,1)} %all_to_all.39, bf16[1536,768,1]{1,0,2:T(8,128)(2,1)S(1)} %bitcast.57), kind=kOutput, calls=%fused_computation.2 | convolution fusion | flops 1813118976 | bytes 7077888 | tf_op jit(solution)/shard_map/sech,edh->secd/dot_general | solution.py:41
  112.7 2.6 %copy.38 = bf16[4,1,96,1536]{2,0,1,3:T(4,128)(2,1)S(1)} copy(bf16[4,1,96,1536]{3,2,0,1:T(8,128)(2,1)} %fusion) | data formatting | bytes 2359296
  115.4 1.9 reshape.69
  117.3 32.7 %reduce-scatter.7.cloned.1.call-done = bf16[192,384]{1,0:T(8,128)(2,1)} async-done(((bf16[1536,384]{1,0:T(8,128)(2,1)}), bf16[192,384]{1,0:T(8,128)(2,1)}) %reduce-scatter.7.cloned.1.call-update) | async-done | bytes 147472
  150.0 1.1 reshape.70
  151.0 0.8 copy.39
  151.9 3.6 %all-to-all-start.3 = ((bf16[4,96,192]{2,1,0:T(8,128)(2,1)}), bf16[4,96,192]{2,1,0:T(8,128)(2,1)S(1)}, u32[]{:S(2)}, u32[]{:S(2)}) async-start(bf16[4,96,192]{2,1,0:T(8,128)(2,1)} %bitcast.13), calls=%async_computation.3 | async-start | bytes 393216 | tf_op jit(solution)/shard_map/all_to_all | solution.py:50
  155.5 5.2 %all-to-all-done.3 = bf16[4,96,192]{2,1,0:T(8,128)(2,1)S(1)} async-done(((bf16[4,96,192]{2,1,0:T(8,128)(2,1)}), bf16[4,96,192]{2,1,0:T(8,128)(2,1)S(1)}, u32[]{:S(2)}, u32[]{:S(2)}) %all-to-all-start.3) | async-done | bytes 147488 | tf_op jit(solution)/shard_map/all_to_all | solution.py:50
  160.7 0.3 convolution_multiply_fusion
  161.0 0.3 fusion.3
  161.3 0.9 convolution_convert_fusion.2
  162.2 27.9 %reduce-scatter.5.cloned.1.call-done = bf16[16,768]{1,0:T(8,128)(2,1)} async-done(((bf16[128,768]{1,0:T(8,128)(2,1)}), bf16[16,768]{1,0:T(8,128)(2,1)}) %reduce-scatter.5.cloned.1.call-update) | async-done | bytes 24592 | tf_op jit(solution)/shard_map/reduce_scatter | solution.py:56
  190.2 0.7 add_maximum_fusion
  191.1 0.7 copy.37
  (35 shorter events, 0.9 us)
Async XLA Ops:
  7.2 154.1 %copy-start = (bf16[192,768]{1,0:T(8,128)(2,1)S(1)}, bf16[192,768]{1,0:T(8,128)(2,1)}, u32[]{:S(2)}) copy-start(bf16[192,768]{1,0:T(8,128)(2,1)} %param.14) | copy-start | bytes 884740
  7.2 142.8 %reduce-scatter.7.cloned.1.call-start = ((), (), s32[]{:S(2)}) async-start(), calls=%async_computation.7 | async-start | bytes 1327104
  27.8 19.8 %copy-start.1 = (bf16[4,384,768]{2,1,0:T(8,128)(2,1)S(1)}, bf16[4,384,768]{2,1,0:T(8,128)(2,1)}, u32[]{:S(2)}) copy-start(bf16[4,384,768]{2,1,0:T(8,128)(2,1)} %param.12) | copy-start | bytes 7077892
  47.6 30.1 %copy-start.2 = (bf16[4,384,768]{2,1,0:T(8,128)(2,1)S(1)}, bf16[4,384,768]{2,1,0:T(8,128)(2,1)}, u32[]{:S(2)}) copy-start(bf16[4,384,768]{2,1,0:T(8,128)(2,1)} %param.13) | copy-start | bytes 7077892
  117.3 38.2 %copy-start.6 = (f32[128,2]{0,1:T(2,128)S(1)}, f32[128,2]{0,1:T(2,128)}, u32[]{:S(2)}) copy-start(f32[128,2]{0,1:T(2,128)} %param.11) | copy-start | bytes 3076
  117.3 72.9 %copy-start.4 = (f32[768]{0:T(1024)S(1)}, f32[768]{0:T(1024)}, u32[]{:S(2)}) copy-start(f32[768]{0:T(1024)} %param.15) | copy-start | bytes 9220
  117.3 73.7 %copy-start.5 = (f32[3,256]{1,0:T(4,128)S(1)}, f32[3,256]{1,0:T(4,128)}, u32[]{:S(2)}) copy-start(f32[3,256]{1,0:T(4,128)} %param.16) | copy-start | bytes 9220
  117.3 73.7 %copy-start.7 = (f32[3]{0:T(128)S(1)}, f32[3]{0:T(128)}, u32[]{:S(2)}) copy-start(f32[3]{0:T(128)} %param.17) | copy-start | bytes 40
  151.9 8.8 %all-to-all-start.3 = ((bf16[4,96,192]{2,1,0:T(8,128)(2,1)}), bf16[4,96,192]{2,1,0:T(8,128)(2,1)S(1)}, u32[]{:S(2)}, u32[]{:S(2)}) async-start(bf16[4,96,192]{2,1,0:T(8,128)(2,1)} %bitcast.13), calls=%async_computation.3 | async-start | bytes 393216 | tf_op jit(solution)/shard_map/all_to_all | solution.py:50
  155.5 34.7 %reduce-scatter.5.cloned.1.call-start = ((), (), s32[]{:S(2)}) async-start(), calls=%async_computation.6 | async-start | bytes 221184 | tf_op jit(solution)/shard_map/reduce_scatter | solution.py:56
  161.3 30.5 %copy-start.3 = (bf16[128,192]{0,1:T(8,128)(2,1)}, bf16[128,192]{0,1:T(8,128)(2,1)S(1)}, u32[]{:S(2)}) copy-start(bf16[128,192]{0,1:T(8,128)(2,1)S(1)} %fusion.3) | copy-start | bytes 147460
Sparse Core Ops, SparseCore 0:
  117.4 32.5 reduce-scatter.6
  162.4 27.7 reduce-scatter.4
where the time goes:
time: 199 us
  blocking collectives  95.8 us (48%)
  waiting for transfers between devices  65.8 us (33%)
  between operations  14.2 us (7%)
  local copies, waits for them, and re-layouts  8.73 us (4%)
  matrix products  7.42 us (4%)
  starting transfers between devices  3.68 us (2%)
  other arithmetic  2.92 us (1%)
    unnamed x3, waiting for transfers between devices  32.7 us
    all_to_all x1, blocking collectives, per_device(): lax.all_to_all(w_up, 'expert', split_axis=0, concat_axis=1, tiled=True)  30.1 us
    all_to_all x1, blocking collectives, per_device(): lax.all_to_all(w_down, 'expert', split_axis=0, concat_axis=1, tiled=True)  29.5 us
    reduce_scatter x1, waiting for transfers between devices, per_device(): lax.psum_scatter(jnp.dot(mixed, tower_in, preferred_element_type=jnp.floa...  27.9 us
    all_to_all x1, blocking collectives, per_device(): lax.all_to_all(outgoing, 'expert', split_axis=0, concat_axis=0, tiled=True)  19.8 us
    all_gather x1, blocking collectives, per_device(): full_rows = lax.all_gather(requests, ('tensor', 'rep'), axis=1, tiled=True)  16.4 us
    unnamed x22, local copies, waits for them, and re-layouts  7.94 us
    dot_general x1, matrix products, per_device(): jnp.einsum('sech,edh->secd', hidden, serve_down, preferred_element_type=j...  5.47 us
  transfers between devices with their start and end apart: 3, of which 3 were waited for; matrix products, arithmetic and copies ran while one was open for 0% of the time, Pallas kernels for 0%

commit v1 on v0

--- a/solution.py
+++ b/solution.py
@@ -1,7 +1,40 @@
+import functools
 import jax
 import jax.numpy as jnp
 from jax import lax
 from jax.sharding import PartitionSpec as P
+
+
+def reach_the_body(state, along_dim, load):
+    u1, earlier = (state.shape[:along_dim], state.shape[along_dim + 1 :])
+    back = state.reshape(*u1, load, -1, *earlier)
+    return jnp.moveaxis(back, along_dim, 0)
+
+
+def divide_turns(values, ndim_at):
+    values = jnp.moveaxis(values, 0, ndim_at)
+    y = values.shape
+    return values.reshape(*y[:ndim_at], y[ndim_at] * y[ndim_at + 1], *y[ndim_at + 2 :])
+
+
+def slices_reach(a0, bus_axis, field_in, q_in):
+    taken_in = lax.axis_size(bus_axis)
+    carry_out = lax.axis_index(bus_axis)
+    aux, d_next = (taken_in, carry_out)
+    e_now = reach_the_body(a0, field_in, aux)
+    history = [e_now[d_next]]
+    b = 1
+    while b < aux:
+        r1 = e_now[d_next ^ b]
+        step_out = lax.ppermute(r1, bus_axis, [(k0, k0 ^ b) for k0 in range(aux)])
+        history.append(step_out)
+        b += 1
+    last = jnp.stack(history)
+    e_now = last[d_next ^ jnp.arange(aux)]
+    return divide_turns(e_now, q_in)
+
+
+remake_the_pieces_all = functools.partial(slices_reach, bus_axis="expert", field_in=0, q_in=0)
 
 
 def tower_head(pre, tower_bias, tower_out, out_bias):
@@ -34,7 +67,7 @@
     ).astype(jnp.bfloat16)
     full_rows = lax.all_gather(requests, ("tensor", "rep"), axis=1, tiled=True)
     outgoing = jnp.dot(spread, full_rows, preferred_element_type=jnp.float32).astype(jnp.bfloat16)
-    incoming = lax.all_to_all(outgoing, "expert", split_axis=0, concat_axis=0, tiled=True)
+    incoming = remake_the_pieces_all(outgoing)
     shaped = incoming.reshape(groups, local_experts, capacity, incoming.shape[1])
     hidden_pre = jnp.einsum("secd,edh->sech", shaped, serve_up, preferred_element_type=jnp.float32)
     hidden = jax.nn.relu(hidden_pre).astype(jnp.bfloat16)

time: 199 us -> 177 us (0.89)
  blocking collectives: 95.8 us -> 15 us
  waiting for transfers between devices: 65.8 us -> 113 us
  starting transfers between devices: 3.68 us -> 17 us
    all_to_all x3 -> x0, blocking collectives: 79.4 us -> none  [the longest x1 30.1 us: per_device(): lax.all_to_all(w_up, 'expert', split_axis=0, concat_axis=1, tiled=True)]
    all_to_all x0 -> x2, waiting for transfers between devices: none -> 25.6 us  [the longest x1 25.6 us: per_device(): lax.all_to_all(w_up, 'expert', split_axis=0, concat_axis=1, tiled=True)]
    ppermute x0 -> x3, waiting for transfers between devices: none -> 20.4 us  [slices_reach(): step_out = lax.ppermute(r1, bus_axis, [(k0, k0 ^ b) for k0 in range(aux)])]
    all_to_all x0 -> x2, starting transfers between devices: none -> 9.83 us  [the longest x1 5.34 us: per_device(): lax.all_to_all(w_up, 'expert', split_axis=0, concat_axis=1, tiled=True)]
    ppermute x0 -> x3, starting transfers between devices: none -> 3.55 us  [slices_reach(): step_out = lax.ppermute(r1, bus_axis, [(k0, k0 ^ b) for k0 in range(aux)])]
    unnamed x22 -> x24, local copies, waits for them, and re-layouts: 7.94 us -> 7.09 us
  transfers between devices with their start and end apart: 3 -> 8, of which waited for: 3 -> 6; matrix products, arithmetic and copies ran while one was open for 0% -> 2% of each run, Pallas kernels for 0% -> 0%
where the time goes in v1:
time: 177 us
  waiting for transfers between devices  113 us (64%)
  starting transfers between devices  17 us (10%)
  blocking collectives  15 us (8%)
  between operations  14.2 us (8%)
  local copies, waits for them, and re-layouts  8.59 us (5%)
  matrix products  6.74 us (4%)
  other arithmetic  2.38 us (1%)
    unnamed x3, waiting for transfers between devices  33.6 us
    reduce_scatter x1, waiting for transfers between devices, per_device(): lax.psum_scatter(jnp.dot(mixed, tower_in, preferred_element_type=jnp.floa...  27.9 us
    all_to_all x1, waiting for transfers between devices, per_device(): lax.all_to_all(w_up, 'expert', split_axis=0, concat_axis=1, tiled=True)  25.6 us
    ppermute x3, waiting for transfers between devices, slices_reach(): step_out = lax.ppermute(r1, bus_axis, [(k0, k0 ^ b) for k0 in range(aux)])  20.4 us
    all_gather x1, blocking collectives, per_device(): full_rows = lax.all_gather(requests, ('tensor', 'rep'), axis=1, tiled=True)  15 us
    unnamed x24, local copies, waits for them, and re-layouts  7.09 us
    all_to_all x1, starting transfers between devices, per_device(): lax.all_to_all(w_up, 'expert', split_axis=0, concat_axis=1, tiled=True)  5.34 us
    all_to_all x1, waiting for transfers between devices, per_device(): lax.all_to_all(expert_out, 'expert', split_axis=0, concat_axis=0, tiled=T...  5.18 us
  transfers between devices with their start and end apart: 8, of which 6 were waited for; matrix products, arithmetic and copies ran while one was open for 2% of the time, Pallas kernels for 0%

profile of v1, /device:TPU:0, one launch (start us, length us, event | category | flops | bytes accessed | tf_op | source)
XLA Modules:
  0.0 176.7 jit_solution(4703577674723129958)
XLA Ops:
  7.2 5.3 %all-to-all-start = ((bf16[4,384,768]{2,1,0:T(8,128)(2,1)}), bf16[4,384,768]{2,1,0:T(8,128)(2,1)S(1)}, u32[]{:S(2)}, u32[]{:S(2)}) async-start(bf16[4,384,768]{2,1,0:T(8,128)(2,1)} %param.12), calls=%async_computation | async-start | bytes 4718592 | tf_op jit(solution)/shard_map/all_to_all | solution.py:56
  12.9 1.2 reduce-window.6
  14.6 25.6 %all-to-all-done = bf16[4,384,768]{2,1,0:T(8,128)(2,1)S(1)} async-done(((bf16[4,384,768]{2,1,0:T(8,128)(2,1)}), bf16[4,384,768]{2,1,0:T(8,128)(2,1)S(1)}, u32[]{:S(2)}, u32[]{:S(2)}) %all-to-all-start) | async-done | bytes 2359328 | tf_op jit(solution)/shard_map/all_to_all | solution.py:56
  40.2 1.4 copy-done.1
  41.6 4.5 %all-to-all-start.1 = ((bf16[4,384,768]{2,1,0:T(8,128)(2,1)}), bf16[4,384,768]{2,1,0:T(8,128)(2,1)}, u32[]{:S(2)}, u32[]{:S(2)}) async-start(bf16[4,384,768]{2,1,0:T(8,128)(2,1)} %param.13), calls=%async_computation.1 | async-start | bytes 4718592 | tf_op jit(solution)/shard_map/all_to_all | solution.py:57
  46.4 15.0 %all_gather.3 = bf16[128,1536]{0,1:T(8,128)(2,1)S(1)} all-gather(bf16[128,192]{0,1:T(8,128)(2,1)S(1)} %copy-done.3), channel_id=1, replica_groups=mesh['expert'=4,'tensor'=4,'rep'=2] {'tensor','rep'}, dimensions={1}, use_global_device_ids=true | all-gather | bytes 442368 | tf_op jit(solution)/shard_map/all_gather | solution.py:68
  61.4 0.5 convolution_convert_fusion
  61.9 2.9 %collective-permute-start.2 = (bf16[96,1536]{1,0:T(8,128)(2,1)S(1)}, bf16[96,1536]{1,0:T(8,128)(2,1)S(1)}, u32[]{:S(2)}, u32[]{:S(2)}) collective-permute-start(bf16[96,1536]{1,0:T(8,128)(2,1)S(1)} %get-tuple-element.7), channel_id=1, source_target_pairs={{0,24},{8,16},{16,8},{24,0},{1,25},{9,17},{17,9},{25,1},{2,26},{10... | collective-permute-start | bytes 884744 | tf_op jit(solution)/shard_map/ppermute | solution.py:29
  64.8 0.6 collective-permute-start
  65.5 16.9 %collective-permute-done.2 = bf16[96,1536]{1,0:T(8,128)(2,1)S(1)} collective-permute-done((bf16[96,1536]{1,0:T(8,128)(2,1)S(1)}, bf16[96,1536]{1,0:T(8,128)(2,1)S(1)}, u32[]{:S(2)}, u32[]{:S(2)}) %collective-permute-start.2) | collective-permute-done | bytes 294944 | tf_op jit(solution)/shard_map/ppermute | solution.py:29
  82.4 3.6 %collective-permute-done = bf16[96,1536]{1,0:T(8,128)(2,1)S(1)} collective-permute-done((bf16[96,1536]{1,0:T(8,128)(2,1)S(1)}, bf16[96,1536]{1,0:T(8,128)(2,1)S(1)}, u32[]{:S(2)}, u32[]{:S(2)}) %collective-permute-start) | collective-permute-done | bytes 294944 | tf_op jit(solution)/shard_map/ppermute | solution.py:29
  86.1 0.6 gather_fusion
  86.8 4.8 %fusion = bf16[4,1,96,1536]{3,2,0,1:T(8,128)(2,1)S(1)} fusion(bf16[1536,768,1]{1,0,2:T(8,128)(2,1)} %bitcast.16, bf16[4,96,1536]{2,1,0:T(8,128)(2,1)S(1)} %gather_fusion, bf16[1536,768,1]{1,0,2:T(8,128)(2,1)} %bitcast.68), kind=kOutput, calls=%fused_computation.3 | convolution fusion | flops 1813118976 | bytes 7077888 | tf_op jit(solution)/shard_map/sech,edh->secd/dot_general | solution.py:74
  91.6 1.1 copy.38
  92.6 1.9 %reshape.93 = bf16[1536,384]{1,0:T(8,128)(2,1)} reshape(bf16[1536,1,4,96]{3,2,1,0:T(4,128)(2,1)S(1)} %bitcast.66) | data formatting | bytes 2359296
  94.6 33.6 %reduce-scatter.7.cloned.1.call-done = bf16[192,384]{1,0:T(8,128)(2,1)} async-done(((bf16[1536,384]{1,0:T(8,128)(2,1)}), bf16[192,384]{1,0:T(8,128)(2,1)}) %reduce-scatter.7.cloned.1.call-update) | async-done | bytes 147472
  128.2 1.1 reshape.94
  129.3 0.8 copy.39
  130.1 3.6 %all-to-all-start.2 = ((bf16[4,96,192]{2,1,0:T(8,128)(2,1)}), bf16[4,96,192]{2,1,0:T(8,128)(2,1)S(1)}, u32[]{:S(2)}, u32[]{:S(2)}) async-start(bf16[4,96,192]{2,1,0:T(8,128)(2,1)} %bitcast.20), calls=%async_computation.2 | async-start | bytes 393216 | tf_op jit(solution)/shard_map/all_to_all | solution.py:83
  133.7 5.2 %all-to-all-done.2 = bf16[4,96,192]{2,1,0:T(8,128)(2,1)S(1)} async-done(((bf16[4,96,192]{2,1,0:T(8,128)(2,1)}), bf16[4,96,192]{2,1,0:T(8,128)(2,1)S(1)}, u32[]{:S(2)}, u32[]{:S(2)}) %all-to-all-start.2) | async-done | bytes 147488 | tf_op jit(solution)/shard_map/all_to_all | solution.py:83
  139.5 0.9 convolution_convert_fusion.2
  140.4 27.9 %reduce-scatter.5.cloned.1.call-done = bf16[16,768]{1,0:T(8,128)(2,1)} async-done(((bf16[128,768]{1,0:T(8,128)(2,1)}), bf16[16,768]{1,0:T(8,128)(2,1)}) %reduce-scatter.5.cloned.1.call-update) | async-done | bytes 24592 | tf_op jit(solution)/shard_map/reduce_scatter | solution.py:89
  168.3 0.7 add_maximum_fusion
  169.2 0.7 copy.37
  (49 shorter events, 2.2 us)
Async XLA Ops:
  7.2 132.3 %copy-start = (bf16[192,768]{1,0:T(8,128)(2,1)S(1)}, bf16[192,768]{1,0:T(8,128)(2,1)}, u32[]{:S(2)}) copy-start(bf16[192,768]{1,0:T(8,128)(2,1)} %param.14) | copy-start | bytes 884740
  7.2 5.3 %copy-start.4 = (s32[128,2]{0,1:T(2,128)S(1)}, s32[128,2]{0,1:T(2,128)}, u32[]{:S(2)}) copy-start(s32[128,2]{0,1:T(2,128)} %param.10) | copy-start | bytes 3076
  7.2 33.0 %all-to-all-start = ((bf16[4,384,768]{2,1,0:T(8,128)(2,1)}), bf16[4,384,768]{2,1,0:T(8,128)(2,1)S(1)}, u32[]{:S(2)}, u32[]{:S(2)}) async-start(bf16[4,384,768]{2,1,0:T(8,128)(2,1)} %param.12), calls=%async_computation | async-start | bytes 4718592 | tf_op jit(solution)/shard_map/all_to_all | solution.py:56
  14.6 31.8 %copy-start.3 = (bf16[128,192]{0,1:T(8,128)(2,1)S(1)}, bf16[128,192]{0,1:T(8,128)(2,1)}, u32[]{:S(2)}) copy-start(bf16[128,192]{0,1:T(8,128)(2,1)} %param.9) | copy-start | bytes 147460
  40.2 1.4 copy-start.1
  41.6 45.1 %all-to-all-start.1 = ((bf16[4,384,768]{2,1,0:T(8,128)(2,1)}), bf16[4,384,768]{2,1,0:T(8,128)(2,1)}, u32[]{:S(2)}, u32[]{:S(2)}) async-start(bf16[4,384,768]{2,1,0:T(8,128)(2,1)} %param.13), calls=%async_computation.1 | async-start | bytes 4718592 | tf_op jit(solution)/shard_map/all_to_all | solution.py:57
  46.1 82.1 %reduce-scatter.7.cloned.1.call-start = ((), (), s32[]{:S(2)}) async-start(), calls=%async_computation.6 | async-start | bytes 1327104
  61.9 20.4 %collective-permute-start.2 = (bf16[96,1536]{1,0:T(8,128)(2,1)S(1)}, bf16[96,1536]{1,0:T(8,128)(2,1)S(1)}, u32[]{:S(2)}, u32[]{:S(2)}) collective-permute-start(bf16[96,1536]{1,0:T(8,128)(2,1)S(1)} %get-tuple-element.7), channel_id=1, source_target_pairs={{0,24},{8,16},{16,8},{24,0},{1,25},{9,17},{17,9},{25,1},{2,26},{10... | collective-permute-start | bytes 884744 | tf_op jit(solution)/shard_map/ppermute | solution.py:29
  64.8 21.1 %collective-permute-start = (bf16[96,1536]{1,0:T(8,128)(2,1)S(1)}, bf16[96,1536]{1,0:T(8,128)(2,1)S(1)}, u32[]{:S(2)}, u32[]{:S(2)}) collective-permute-start(bf16[96,1536]{1,0:T(8,128)(2,1)S(1)} %get-tuple-element.9), channel_id=1, source_target_pairs={{0,8},{8,0},{16,24},{24,16},{1,9},{9,1},{17,25},{25,17},{2,10},{10... | collective-permute-start | bytes 884744 | tf_op jit(solution)/shard_map/ppermute | solution.py:29
  65.4 20.6 %collective-permute-start.1 = (bf16[96,1536]{1,0:T(8,128)(2,1)S(1)}, bf16[96,1536]{1,0:T(8,128)(2,1)S(1)}, u32[]{:S(2)}, u32[]{:S(2)}) collective-permute-start(bf16[96,1536]{1,0:T(8,128)(2,1)S(1)} %get-tuple-element.8), channel_id=1, source_target_pairs={{0,16},{8,24},{16,0},{24,8},{1,17},{9,25},{17,1},{25,9},{2,18},{10... | collective-permute-start | bytes 884744 | tf_op jit(solution)/shard_map/ppermute | solution.py:29
  94.5 39.2 %copy-start.7 = (f32[128,2]{0,1:T(2,128)S(1)}, f32[128,2]{0,1:T(2,128)}, u32[]{:S(2)}) copy-start(f32[128,2]{0,1:T(2,128)} %param.11) | copy-start | bytes 3076
  94.6 73.7 %copy-start.5 = (f32[768]{0:T(1024)S(1)}, f32[768]{0:T(1024)}, u32[]{:S(2)}) copy-start(f32[768]{0:T(1024)} %param.15) | copy-start | bytes 9220
  129.2 39.9 %copy-start.6 = (f32[3,256]{1,0:T(4,128)S(1)}, f32[3,256]{1,0:T(4,128)}, u32[]{:S(2)}) copy-start(f32[3,256]{1,0:T(4,128)} %param.16) | copy-start | bytes 9220
  129.2 40.0 %copy-start.8 = (f32[3]{0:T(128)S(1)}, f32[3]{0:T(128)}, u32[]{:S(2)}) copy-start(f32[3]{0:T(128)} %param.17) | copy-start | bytes 40
  130.1 8.8 %all-to-all-start.2 = ((bf16[4,96,192]{2,1,0:T(8,128)(2,1)}), bf16[4,96,192]{2,1,0:T(8,128)(2,1)S(1)}, u32[]{:S(2)}, u32[]{:S(2)}) async-start(bf16[4,96,192]{2,1,0:T(8,128)(2,1)} %bitcast.20), calls=%async_computation.2 | async-start | bytes 393216 | tf_op jit(solution)/shard_map/all_to_all | solution.py:83
  133.7 34.6 %reduce-scatter.5.cloned.1.call-start = ((), (), s32[]{:S(2)}) async-start(), calls=%async_computation.5 | async-start | bytes 221184 | tf_op jit(solution)/shard_map/reduce_scatter | solution.py:89
  139.5 30.4 %copy-start.2 = (bf16[128,192]{0,1:T(8,128)(2,1)}, bf16[128,192]{0,1:T(8,128)(2,1)S(1)}, u32[]{:S(2)}) copy-start(bf16[128,192]{0,1:T(8,128)(2,1)S(1)} %fusion.3) | copy-start | bytes 147460
Sparse Core Ops, SparseCore 0:
  94.7 33.4 reduce-scatter.6
  140.6 27.7 reduce-scatter.4
